TPU v7x, 512 devices: a whole 4x4x16 slice. The times are simulated.
512 devices in a mesh: depth: 4 (over y_hi, core), blk: 128 (over z, x, y_lo).
Axes of the slice: x: 4, y: 4 (y_hi: 2, y_lo: 2; y = y_hi * 2 + y_lo), z: 16, core: 2. Of those that a mesh axis runs over, the one named last changes fastest.
Arguments:
- jacobian: bfloat16 [1536, 16384], P(('depth', 'blk')), may hold values from -6 to 6
- gain_inverse: bfloat16 [16384, 16384], P('depth', 'blk'), may hold values from -0.00024414062 to 0.00048828125, as said below
- variance: float32 [1536], P(('depth', 'blk')), may hold values from 2 to 12
Outputs:
- omega_diag: float32 [1536], P(('depth', 'blk'))
Inputs may be any that keep to these rules, and one draw needn't show every extreme that they name: gain_inverse is symmetric and positive definite.
All inputs are finite; a program needn't handle non-finite values.
Results may differ from a plain program's by a relative error of at most 0.0003.
Values may be sent and summed in bfloat16 or wider, within the bound.
No kernel may reach another device: no remote copies, remote signals or barrier semaphores. Data moves between devices by JAX's collectives and lax.ppermute only.
A program may use at most 128 MiB of HBM per device.

v0:
```python
import jax
import jax.numpy as jnp
from jax import lax
from jax.sharding import Mesh
from jax.sharding import PartitionSpec as P

BLK = ("blk_0", "blk_1", "blk_2")
DEPTH_BLK = ("depth", "blk_0", "blk_1", "blk_2")


def in_order(parts, dim):
    shape = list(parts.shape[1:])
    shape[dim] *= parts.shape[0]
    return jnp.moveaxis(parts, 0, dim).reshape(shape)


def copy_for_each(shard, axis):
    copies = jnp.broadcast_to(shard, (lax.axis_size(axis), *shard.shape))
    return lax.all_to_all(copies, axis, split_axis=0, concat_axis=0, tiled=True)


def collect(shard, axis, dim):
    return in_order(copy_for_each(shard, axis), dim)


def edges_of(length, count):
    unit = 8 if length >= 8 * count else 1
    return [length // unit * k // count * unit for k in range(1, count)]


def gather_in_order(shard, axes, turns):
    parts = shard[None]
    for k in turns:
        parts = lax.all_gather(parts, axes[k], axis=0, tiled=True)
    current = [lax.axis_size(axes[k]) for k in reversed(turns)]
    parts = parts.reshape(*current, *shard.shape)
    turned = sorted(range(len(turns)), key=lambda place: turns[len(turns) - 1 - place])
    return parts.transpose(*turned, *range(len(turns), parts.ndim)).reshape(-1, *shard.shape)


def gather_all_axes(shard, axes, dim):
    numbers = list(range(len(axes)))[::-1]
    cut = shard.shape.index(max(shard.shape[:-1] or shard.shape))
    edges = [0, *edges_of(shard.shape[cut], len(axes)), shard.shape[cut]]
    gathered = []
    for k, (start, end) in enumerate(zip(edges, edges[1:])):
        if end > start:
            slab = lax.slice_in_dim(shard, start, end, axis=cut)
            gathered.append(gather_in_order(slab, axes, numbers[k:] + numbers[:k]))
    return in_order(jnp.concatenate(gathered, axis=cut + 1), dim)


def shards(jacobian, gain_inverse, variance):
    rows_local = jacobian.shape[0]
    width = jacobian.shape[1]
    depth_count = lax.axis_size("depth")
    blk_count = lax.axis_size(BLK)
    panel_width = width // blk_count
    quarter_rows = lax.all_to_all(jacobian, "depth", split_axis=1, concat_axis=0, tiled=True)
    by_blk = lax.all_to_all(jacobian, BLK, split_axis=1, concat_axis=0, tiled=True)
    flat = by_blk.reshape(blk_count, rows_local * panel_width)
    joined = collect(flat, "depth", 1)
    panel = joined.reshape(blk_count * depth_count * rows_local, panel_width)
    gathered = gather_all_axes(quarter_rows, BLK, 0)
    projected = jnp.dot(gathered, gain_inverse, preferred_element_type=jnp.float32)
    partials = jnp.sum(projected * panel.astype(jnp.float32), axis=1)
    ordered = partials.reshape(blk_count, depth_count, rows_local).transpose(1, 0, 2).reshape(-1)
    quadratic = lax.psum_scatter(ordered, DEPTH_BLK, scatter_dimension=0, tiled=True)
    return variance - quadratic


def solution(mesh):
    split = Mesh(
        mesh.devices.reshape(mesh.shape["depth"], 16, 4, 2), ("depth", "blk_0", "blk_1", "blk_2")
    )
    return jax.shard_map(
        shards,
        mesh=split,
        in_specs=(P(DEPTH_BLK, None), P("depth", BLK), P(DEPTH_BLK)),
        out_specs=P(DEPTH_BLK),
        check_vma=False,
    )
```

profile of v0, /device:TPU:1, one launch (start us, length us, event | category | flops | bytes accessed | tf_op | source)
XLA Modules:
  0.0 513.9 jit_solution(17710025762078432333)
XLA Ops:
  6.5 15.3 %all_to_all.40 = bf16[3,4,4096]{2,0,1:T(4,128)(2,1)S(1)} all-to-all(bf16[3,4,4096]{2,0,1:T(4,128)(2,1)} %bitcast.30), channel_id=1, replica_groups=mesh['depth'=4,'blk_0'=16,'blk_1'=4,'blk_2'=2] {'depth'}, dimensions={1} | all-to-all | bytes 196608 | tf_op jit(solution)/shard_map/all_to_all | solution.py:59
  22.0 29.5 %all-gather.5 = bf16[16,4,4096]{2,1,0:T(4,128)(2,1)} all-gather(bf16[1,4,4096]{2,1,0:T(4,128)(2,1)S(1)} %get-tuple-element.6), channel_id=4, replica_groups=mesh['depth'=4,'blk_0'=16,'blk_1'=4,'blk_2'=2] {'blk_0'}, dimensions={0}, use_global_device_ids=true | all-gather | bytes 557056 | tf_op jit(solution)/shard_map/all_gather | solution.py:34
  51.6 10.2 %all-gather.4 = bf16[4,4,4096]{2,1,0:T(4,128)(2,1)} all-gather(bf16[1,4,4096]{2,1,0:T(4,128)(2,1)S(1)} %get-tuple-element.7), channel_id=3, replica_groups=mesh['depth'=4,'blk_0'=16,'blk_1'=4,'blk_2'=2] {'blk_1'}, dimensions={0}, use_global_device_ids=true | all-gather | bytes 163840 | tf_op jit(solution)/shard_map/all_gather | solution.py:34
  61.9 21.9 %all-gather.18.cloned.1.call-done = bf16[32,4,4096]{2,1,0:T(4,128)(2,1)} async-done(((bf16[16,4,4096]{2,1,0:T(4,128)(2,1)}), bf16[32,4,4096]{2,1,0:T(4,128)(2,1)}) %all-gather.18.cloned.1.call-update) | async-done | bytes 1048592 | tf_op jit(solution)/shard_map/all_gather | solution.py:34
  83.8 66.7 %all-gather.14.cloned.1.call-done = bf16[64,4,4096]{2,1,0:T(4,128)(2,1)} async-done(((bf16[4,4,4096]{2,1,0:T(4,128)(2,1)}), bf16[64,4,4096]{2,1,0:T(4,128)(2,1)}) %all-gather.14.cloned.1.call-update) | async-done | bytes 2097168 | tf_op jit(solution)/shard_map/all_gather | solution.py:34
  150.6 3.7 all-gather.3
  154.2 10.6 %all_gather.28 = bf16[8,4,4096]{2,1,0:T(4,128)(2,1)} all-gather(bf16[2,4,4096]{2,1,0:T(4,128)(2,1)S(1)} %all-gather.3), channel_id=1, replica_groups=mesh['depth'=4,'blk_0'=16,'blk_1'=4,'blk_2'=2] {'blk_1'}, dimensions={0}, use_global_device_ids=true | all-gather | bytes 327680 | tf_op jit(solution)/shard_map/all_gather | solution.py:34
  164.8 26.2 %all_to_all.41 = bf16[3,128,128]{2,0,1:T(4,128)(2,1)S(1)} all-to-all(bf16[3,128,128]{2,0,1:T(4,128)(2,1)} %bitcast.31), channel_id=1, replica_groups=mesh['depth'=4,'blk_0'=16,'blk_1'=4,'blk_2'=2] {'blk_0','blk_1','blk_2'}, dimensions={1} | all-to-all | bytes 196608 | tf_op jit(solution)/shard_map/all_to_all | solution.py:60
  191.3 0.8 broadcast_in_dim.15
  192.1 19.0 %all-to-all-start.2 = ((bf16[4,128,384]{2,1,0:T(8,128)(2,1)}), bf16[4,128,384]{2,1,0:T(8,128)(2,1)S(1)}, u32[]{:S(2)}, u32[]{:S(2)}) async-start(bf16[4,128,384]{2,1,0:T(8,128)(2,1)} %broadcast_in_dim.15), calls=%async_computation.2 | async-start | bytes 786432 | tf_op jit(solution)/shard_map/all_to_all | solution.py:19
  211.0 7.9 %all-to-all-done.2 = bf16[4,128,384]{2,1,0:T(8,128)(2,1)S(1)} async-done(((bf16[4,128,384]{2,1,0:T(8,128)(2,1)}), bf16[4,128,384]{2,1,0:T(8,128)(2,1)S(1)}, u32[]{:S(2)}, u32[]{:S(2)}) %all-to-all-start.2) | async-done | bytes 393248 | tf_op jit(solution)/shard_map/all_to_all | solution.py:19
  219.0 0.5 copy.25
  219.5 0.3 reshape.41
  219.9 0.3 copy.26
  220.2 7.9 %copy.21 = bf16[4,2,16,4,4096]{4,3,1,0,2:T(4,128)(2,1)} copy(bf16[4,2,16,4,4096]{4,3,2,1,0:T(4,128)(2,1)} %bitcast.27) | data formatting | bytes 8388608 | tf_op jit(solution)/shard_map/reshape | solution.py:36
  228.0 56.5 %all-gather.16.cloned.1.call-done = bf16[128,4,4096]{2,1,0:T(4,128)(2,1)} async-done(((bf16[64,4,4096]{2,1,0:T(4,128)(2,1)}), bf16[128,4,4096]{2,1,0:T(4,128)(2,1)}) %all-gather.16.cloned.1.call-update) | async-done | bytes 4194320 | tf_op jit(solution)/shard_map/all_gather | solution.py:34
  284.5 7.9 %copy.20 = bf16[2,16,4,4,4096]{4,3,0,2,1:T(4,128)(2,1)} copy(bf16[2,16,4,4,4096]{4,3,2,1,0:T(4,128)(2,1)} %bitcast.28) | data formatting | bytes 8388608 | tf_op jit(solution)/shard_map/reshape | solution.py:36
  292.4 64.5 %all-gather.12.cloned.1.call-done = bf16[128,4,4096]{2,1,0:T(4,128)(2,1)} async-done(((bf16[8,4,4096]{2,1,0:T(4,128)(2,1)}), bf16[128,4,4096]{2,1,0:T(4,128)(2,1)}) %all-gather.12.cloned.1.call-update) | async-done | bytes 4194320 | tf_op jit(solution)/shard_map/all_gather | solution.py:34
  356.9 12.1 %pad_maximum_fusion = bf16[128,12,4096]{2,1,0:T(8,128)(2,1)} fusion(bf16[128,4,4096]{2,1,0:T(4,128)(2,1)} %bitcast.25, bf16[128,4,4096]{2,1,0:T(4,128)(2,1)} %bitcast.26, bf16[128,4,4096]{2,1,0:T(4,128)(2,1)} %all-gather.12.cloned.1.call-done), kind=kLoop, calls=%fused_computation | loop fusion | flops 37748736 | bytes 25165824 | tf_op jit(solution)/shard_map/concatenate | solution.py:50
  369.0 18.1 %reshape.37 = bf16[1536,4096]{1,0:T(8,128)(2,1)} reshape(bf16[128,12,4096]{2,1,0:T(8,128)(2,1)} %pad_maximum_fusion) | data formatting | bytes 25165824 | tf_op jit(solution)/shard_map/reshape | solution.py:14
  387.1 8.9 %fusion = f32[1536]{0:T(1024)S(1)} fusion(f32[1536,128]{0,1:T(8,128)S(1)} %copy.26, bf16[1536,4096]{1,0:T(8,128)(2,1)} %reshape.37, bf16[4096,128]{1,0:T(8,128)(2,1)S(1)} %copy-done), kind=kOutput, calls=%fused_computation.2 | convolution fusion | flops 1611004416 | bytes 14424064 | tf_op jit(solution)/shard_map/dot_general | solution.py:65
  396.1 0.3 reshape.39
  396.6 110.2 %all-reduce = f32[1536]{0:T(1024)S(1)} all-reduce(f32[1536]{0:T(1024)S(1)} %reshape.40), channel_id=5, replica_groups=mesh['depth'=4,'blk_0'=16,'blk_1'=4,'blk_2'=2] {'depth','blk_0','blk_1',..., use_global_device_ids=true, to_apply=%region_1.0.clone | all-reduce | flops 1536 | bytes 12288
  506.8 0.6 dynamic-slice_subtract_fusion
  (22 shorter events, 0.9 us)
Async XLA Ops:
  6.5 380.6 %copy-start = (bf16[4096,128]{1,0:T(8,128)(2,1)S(1)}, bf16[4096,128]{1,0:T(8,128)(2,1)}, u32[]{:S(2)}) copy-start(bf16[4096,128]{1,0:T(8,128)(2,1)} %param.4) | copy-start | bytes 3145732
  6.5 77.2 %all-gather.18.cloned.1.call-start = ((), (), s32[]{:S(2)}) async-start(), calls=%async_computation.6 | async-start | bytes 1572864 | tf_op jit(solution)/shard_map/all_gather | solution.py:34
  51.6 98.9 %all-gather.14.cloned.1.call-start = ((), (), s32[]{:S(2)}) async-start(), calls=%async_computation.4 | async-start | bytes 2228224 | tf_op jit(solution)/shard_map/all_gather | solution.py:34
  61.8 158.3 %all-gather.20.cloned.1.call-start = ((), (), s32[]{:S(2)}) async-start(), calls=%async_computation.7 | async-start | bytes 5242880 | tf_op jit(solution)/shard_map/all_gather | solution.py:34
  83.8 200.7 %all-gather.16.cloned.1.call-start = ((), (), s32[]{:S(2)}) async-start(), calls=%async_computation.5 | async-start | bytes 6291456 | tf_op jit(solution)/shard_map/all_gather | solution.py:34
  150.5 206.4 %all-gather.12.cloned.1.call-start = ((), (), s32[]{:S(2)}) async-start(), calls=%async_computation.3 | async-start | bytes 4456448 | tf_op jit(solution)/shard_map/all_gather | solution.py:34
  192.1 26.9 %all-to-all-start.2 = ((bf16[4,128,384]{2,1,0:T(8,128)(2,1)}), bf16[4,128,384]{2,1,0:T(8,128)(2,1)S(1)}, u32[]{:S(2)}, u32[]{:S(2)}) async-start(bf16[4,128,384]{2,1,0:T(8,128)(2,1)} %broadcast_in_dim.15), calls=%async_computation.2 | async-start | bytes 786432 | tf_op jit(solution)/shard_map/all_to_all | solution.py:19
  387.1 119.6 %copy-start.1 = (f32[3]{0:T(128)S(1)}, f32[3]{0:T(128)}, u32[]{:S(2)}) copy-start(f32[3]{0:T(128)} %param.5) | copy-start | bytes 40
Sparse Core Ops, SparseCore 0:
  51.7 32.0 all-gather.17
  85.8 64.6 all-gather.13
  152.6 63.1 all-gather.19
  217.7 66.7 all-gather.15
  286.4 70.4 all-gather.11
where the time goes:
time: 515 us; the launch traced here: 514 us
  waiting for transfers between devices  218 us (42%)
  blocking collectives  206 us (40%)
  local copies, waits for them, and re-layouts  36.6 us (7%)
  starting transfers between devices  19.1 us (4%)
  between operations  13.2 us (3%)
  other arithmetic  12.8 us (2%)
  matrix products  8.9 us (2%)
    all_gather x5, waiting for transfers between devices, gather_in_order(): parts = lax.all_gather(parts, axes[k], axis=0, tiled=True)  210 us
    unnamed x1, blocking collectives  110 us
    all_gather x4, blocking collectives, gather_in_order(): parts = lax.all_gather(parts, axes[k], axis=0, tiled=True)  54 us
    all_to_all x1, blocking collectives, shards(): lax.all_to_all(jacobian, BLK, split_axis=1, concat_axis=0, tiled=True)  26.2 us
    all_to_all x1, starting transfers between devices, copy_for_each(): return lax.all_to_all(copies, axis, split_axis=0, concat_axis=0, tiled=True)  19 us
    reshape x1, local copies, waits for them, and re-layouts, in_order(): return jnp.moveaxis(parts, 0, dim).reshape(shape)  18.1 us
    reshape x2, local copies, waits for them, and re-layouts, gather_in_order(): parts = parts.reshape(*current, *shard.shape)  15.7 us
    all_to_all x1, blocking collectives, shards(): lax.all_to_all(jacobian, 'depth', split_axis=1, concat_axis=0, tiled=True)  15.3 us
  transfers between devices with their start and end apart: 6, of which 5 were waited for; matrix products, arithmetic and copies ran while one was open for 3% of the time, Pallas kernels for 0%

commit v1 on v0

--- a/solution.py
+++ b/solution.py
@@ -31,7 +31,9 @@
 def gather_in_order(shard, axes, turns):
     parts = shard[None]
     for k in turns:
-        parts = lax.all_gather(parts, axes[k], axis=0, tiled=True)
+        parts = jnp.concatenate(
+            lax.all_to_all(jnp.stack([parts] * lax.axis_size(axes[k])), axes[k], 0, 0), axis=0
+        )
     current = [lax.axis_size(axes[k]) for k in reversed(turns)]
     parts = parts.reshape(*current, *shard.shape)
     turned = sorted(range(len(turns)), key=lambda place: turns[len(turns) - 1 - place])

time: 515 us -> 681 us (1.32)
  waiting for transfers between devices: 218 us -> 326 us
  starting transfers between devices: 19.1 us -> 47.9 us
  blocking collectives: 206 us -> 233 us
  between operations: 13.2 us -> 0.17 us
  local copies, waits for them, and re-layouts: 36.6 us -> 46.6 us
    all_to_all x0 -> x4, waiting for transfers between devices: none -> 319 us  [gather_in_order(): lax.all_to_all(jnp.stack([parts] * lax.axis_size(axes[k])), axes[k], 0, 0)]
    all_gather x5 -> x0, waiting for transfers between devices: 210 us -> none  [gather_in_order(): parts = lax.all_gather(parts, axes[k], axis=0, tiled=True)]
    all_to_all x0 -> x5, blocking collectives: none -> 86.2 us  [gather_in_order(): lax.all_to_all(jnp.stack([parts] * lax.axis_size(axes[k])), axes[k], 0, 0)]
    all_gather x4 -> x0, blocking collectives: 54 us -> none  [gather_in_order(): parts = lax.all_gather(parts, axes[k], axis=0, tiled=True)]
    all_to_all x0 -> x4, starting transfers between devices: none -> 35.8 us  [gather_in_order(): lax.all_to_all(jnp.stack([parts] * lax.axis_size(axes[k])), axes[k], 0, 0)]
    another operation x0 -> x9, local copies, waits for them, and re-layouts: none -> 15.8 us  [the longest x8 11.9 us: gather_in_order(): jnp.stack([parts] * lax.axis_size(axes[k]))]
    reshape x2 -> x0, local copies, waits for them, and re-layouts: 15.7 us -> none  [gather_in_order(): parts = parts.reshape(*current, *shard.shape)]
    unnamed x1, blocking collectives: 110 us -> 102 us
  transfers between devices with their start and end apart: 6 -> 5, of which waited for: 5 -> 5; matrix products, arithmetic and copies ran while one was open for 3% -> 3% of each run, Pallas kernels for 0% -> 0%
where the time goes in v1:
time: 681 us; the launch traced here: 679 us
  waiting for transfers between devices  326 us (48%)
  blocking collectives  233 us (34%)
  starting transfers between devices  47.9 us (7%)
  local copies, waits for them, and re-layouts  46.6 us (7%)
  other arithmetic  17.1 us (3%)
  matrix products  8.9 us (1%)
    all_to_all x4, waiting for transfers between devices, gather_in_order(): lax.all_to_all(jnp.stack([parts] * lax.axis_size(axes[k])), axes[k], 0, 0)  319 us
    unnamed x1, blocking collectives  102 us
    all_to_all x5, blocking collectives, gather_in_order(): lax.all_to_all(jnp.stack([parts] * lax.axis_size(axes[k])), axes[k], 0, 0)  86.2 us
    all_to_all x4, starting transfers between devices, gather_in_order(): lax.all_to_all(jnp.stack([parts] * lax.axis_size(axes[k])), axes[k], 0, 0)  35.8 us
    all_to_all x1, blocking collectives, shards(): lax.all_to_all(jacobian, BLK, split_axis=1, concat_axis=0, tiled=True)  28.7 us
    reshape x1, local copies, waits for them, and re-layouts, in_order(): return jnp.moveaxis(parts, 0, dim).reshape(shape)  18.1 us
    all_to_all x1, blocking collectives, shards(): lax.all_to_all(jacobian, 'depth', split_axis=1, concat_axis=0, tiled=True)  15.3 us
  transfers between devices with their start and end apart: 5, of which 5 were waited for; matrix products, arithmetic and copies ran while one was open for 3% of the time, Pallas kernels for 0%

profile of v1, /device:TPU:1, one launch (start us, length us, event | category | flops | bytes accessed | tf_op | source)
XLA Modules:
  0.0 679.4 jit_solution(11067693507656661145)
XLA Ops:
  0.0 15.3 %all_to_all.85 = bf16[3,4,4096]{2,0,1:T(4,128)(2,1)S(1)} all-to-all(bf16[3,4,4096]{2,0,1:T(4,128)(2,1)} %bitcast.37), channel_id=1, replica_groups=mesh['depth'=4,'blk_0'=16,'blk_1'=4,'blk_2'=2] {'depth'}, dimensions={1} | all-to-all | bytes 196608 | tf_op jit(solution)/shard_map/all_to_all | solution.py:61
  15.5 5.3 all_to_all.86
  20.9 7.2 %all_to_all.87 = bf16[4,1,4,4096]{3,2,1,0:T(4,128)(2,1)S(1)} all-to-all(bf16[4,1,4,4096]{3,2,1,0:T(4,128)(2,1)S(1)} %stack.30), channel_id=1, replica_groups=mesh['depth'=4,'blk_0'=16,'blk_1'=4,'blk_2'=2] {'blk_1'}, dimensions={0} | all-to-all | bytes 262144 | tf_op jit(solution)/shard_map/all_to_all | solution.py:35
  28.2 8.6 %all_to_all.88 = bf16[4,2,4,4096]{3,2,1,0:T(4,128)(2,1)} all-to-all(bf16[4,2,4,4096]{3,2,1,0:T(4,128)(2,1)S(1)} %stack.28), channel_id=1, replica_groups=mesh['depth'=4,'blk_0'=16,'blk_1'=4,'blk_2'=2] {'blk_1'}, dimensions={0} | all-to-all | bytes 524288 | tf_op jit(solution)/shard_map/all_to_all | solution.py:35
  36.8 28.7 %all_to_all.89 = bf16[3,128,128]{2,0,1:T(4,128)(2,1)S(1)} all-to-all(bf16[3,128,128]{2,0,1:T(4,128)(2,1)} %bitcast.38), channel_id=1, replica_groups=mesh['depth'=4,'blk_0'=16,'blk_1'=4,'blk_2'=2] {'blk_0','blk_1','blk_2'}, dimensions={1} | all-to-all | bytes 196608 | tf_op jit(solution)/shard_map/all_to_all | solution.py:62
  66.4 4.2 all-to-all-start.7
  70.9 20.3 %all-to-all-done.7 = bf16[16,1,4,4096]{3,2,1,0:T(4,128)(2,1)S(1)} async-done(((bf16[16,1,4,4096]{3,2,1,0:T(4,128)(2,1)}), bf16[16,1,4,4096]{3,2,1,0:T(4,128)(2,1)S(1)}, u32[]{:S(2)}, u32[]{:S(2)}) %all-to-all-start.7) | async-done | bytes 524320 | tf_op jit(solution)/shard_map/all_to_all | solution.py:35
  92.0 12.1 %all-to-all-start.11 = ((bf16[4,128,384]{2,1,0:T(8,128)(2,1)}), bf16[4,128,384]{2,1,0:T(8,128)(2,1)S(1)}, u32[]{:S(2)}, u32[]{:S(2)}) async-start(bf16[4,128,384]{2,1,0:T(8,128)(2,1)} %broadcast_in_dim.3), calls=%async_computation.11 | async-start | bytes 786432 | tf_op jit(solution)/shard_map/all_to_all | solution.py:19
  105.1 6.9 %all-to-all-done.11 = bf16[4,128,384]{2,1,0:T(8,128)(2,1)S(1)} async-done(((bf16[4,128,384]{2,1,0:T(8,128)(2,1)}), bf16[4,128,384]{2,1,0:T(8,128)(2,1)S(1)}, u32[]{:S(2)}, u32[]{:S(2)}) %all-to-all-start.11) | async-done | bytes 393248 | tf_op jit(solution)/shard_map/all_to_all | solution.py:19
  112.0 15.9 %all_to_all.90 = bf16[2,16,4,4096]{3,1,2,0:T(8,128)(2,1)} all-to-all(bf16[2,16,4,4096]{3,1,2,0:T(8,128)(2,1)S(1)} %copy.26), channel_id=1, replica_groups=mesh['depth'=4,'blk_0'=16,'blk_1'=4,'blk_2'=2] {'blk_2'}, dimensions={0} | all-to-all | bytes 2097152 | tf_op jit(solution)/shard_map/all_to_all | solution.py:35
  130.3 6.8 %all-to-all-start.5 = ((bf16[16,4,4,4096]{3,2,1,0:T(4,128)(2,1)}), bf16[16,4,4,4096]{3,2,1,0:T(4,128)(2,1)S(1)}, u32[]{:S(2)}, u32[]{:S(2)}) async-start(bf16[16,4,4,4096]{3,2,1,0:T(4,128)(2,1)} %stack.31), calls=%async_computation.5 | async-start | bytes 4194304 | tf_op jit(solution)/shard_map/all_to_all | solution.py:35
  139.4 89.6 %all-to-all-done.5 = bf16[16,4,4,4096]{3,2,1,0:T(4,128)(2,1)S(1)} async-done(((bf16[16,4,4,4096]{3,2,1,0:T(4,128)(2,1)}), bf16[16,4,4,4096]{3,2,1,0:T(4,128)(2,1)S(1)}, u32[]{:S(2)}, u32[]{:S(2)}) %all-to-all-start.5) | async-done | bytes 2097184 | tf_op jit(solution)/shard_map/all_to_all | solution.py:35
  232.7 4.8 all-to-all-start.9
  241.4 40.2 %all-to-all-done.9 = bf16[4,32,4,4096]{3,1,2,0:T(8,128)(2,1)} async-done(((bf16[4,32,4,4096]{3,1,2,0:T(8,128)(2,1)}), bf16[4,32,4,4096]{3,1,2,0:T(8,128)(2,1)}, u32[]{:S(2)}, u32[]{:S(2)}) %all-to-all-start.9) | async-done | bytes 4194336 | tf_op jit(solution)/shard_map/all_to_all | solution.py:35
  281.6 49.1 %all_to_all.91 = bf16[2,64,4,4096]{3,2,1,0:T(4,128)(2,1)} all-to-all(bf16[2,64,4,4096]{3,2,1,0:T(4,128)(2,1)} %pad_maximum_fusion.1), channel_id=1, replica_groups=mesh['depth'=4,'blk_0'=16,'blk_1'=4,'blk_2'=2] {'blk_2'}, dimensions={0} | all-to-all | bytes 8388608 | tf_op jit(solution)/shard_map/all_to_all | solution.py:35
  330.7 4.1 stack.29
  334.7 20.0 %all-to-all-start.3 = ((bf16[16,8,4,4096]{3,2,1,0:T(4,128)(2,1)}), bf16[16,8,4,4096]{3,2,1,0:T(4,128)(2,1)}, u32[]{:S(2)}, u32[]{:S(2)}) async-start(bf16[16,8,4,4096]{3,2,1,0:T(4,128)(2,1)} %stack.29), calls=%async_computation.3 | async-start | bytes 8388608 | tf_op jit(solution)/shard_map/all_to_all | solution.py:35
  355.9 7.5 %copy.28 = bf16[16,4,2,4,4096]{4,3,2,1,0:T(4,128)(2,1)} copy(bf16[16,4,2,4,4096]{4,0,2,3,1:T(8,128)(2,1)} %bitcast.14) | data formatting | bytes 8388608 | tf_op jit(solution)/shard_map/transpose | solution.py:40
  363.5 4.0 copy.25
  367.5 169.1 %all-to-all-done.3 = bf16[16,8,4,4096]{3,2,1,0:T(4,128)(2,1)} async-done(((bf16[16,8,4,4096]{3,2,1,0:T(4,128)(2,1)}), bf16[16,8,4,4096]{3,2,1,0:T(4,128)(2,1)}, u32[]{:S(2)}, u32[]{:S(2)}) %all-to-all-start.3) | async-done | bytes 4194336 | tf_op jit(solution)/shard_map/all_to_all | solution.py:35
  536.6 12.1 %pad_maximum_fusion = bf16[128,12,4096]{2,1,0:T(8,128)(2,1)} fusion(bf16[128,4,4096]{2,1,0:T(4,128)(2,1)} %bitcast.28, bf16[128,4,4096]{2,1,0:T(4,128)(2,1)} %bitcast.29, bf16[128,4,4096]{2,1,0:T(4,128)(2,1)} %bitcast.5), kind=kLoop, calls=%fused_computation | loop fusion | flops 37748736 | bytes 25165824 | tf_op jit(solution)/shard_map/concatenate | solution.py:52
  548.7 18.1 %reshape.41 = bf16[1536,4096]{1,0:T(8,128)(2,1)} reshape(bf16[128,12,4096]{2,1,0:T(8,128)(2,1)} %pad_maximum_fusion) | data formatting | bytes 25165824 | tf_op jit(solution)/shard_map/reshape | solution.py:14
  566.9 8.9 %fusion = f32[1536]{0:T(1024)S(1)} fusion(f32[1536,128]{0,1:T(8,128)S(1)} %copy.33, bf16[1536,4096]{1,0:T(8,128)(2,1)} %reshape.41, bf16[4096,128]{1,0:T(8,128)(2,1)S(1)} %copy-done), kind=kOutput, calls=%fused_computation.3 | convolution fusion | flops 1611004416 | bytes 14424064 | tf_op jit(solution)/shard_map/dot_general | solution.py:67
  576.3 102.5 %all-reduce = f32[1536]{0:T(1024)S(1)} all-reduce(f32[1536]{0:T(1024)S(1)} %reshape.44), channel_id=2, replica_groups=mesh['depth'=4,'blk_0'=16,'blk_1'=4,'blk_2'=2] {'depth','blk_0','blk_1',..., use_global_device_ids=true, to_apply=%region_1.0.clone | all-reduce | flops 1536 | bytes 12288
  (31 shorter events, 17.8 us)
Async XLA Ops:
  0.0 566.9 %copy-start = (bf16[4096,128]{1,0:T(8,128)(2,1)S(1)}, bf16[4096,128]{1,0:T(8,128)(2,1)}, u32[]{:S(2)}) copy-start(bf16[4096,128]{1,0:T(8,128)(2,1)} %param.4) | copy-start | bytes 3145732
  66.4 24.8 %all-to-all-start.7 = ((bf16[16,1,4,4096]{3,2,1,0:T(4,128)(2,1)}), bf16[16,1,4,4096]{3,2,1,0:T(4,128)(2,1)S(1)}, u32[]{:S(2)}, u32[]{:S(2)}) async-start(bf16[16,1,4,4096]{3,2,1,0:T(4,128)(2,1)} %stack.33), calls=%async_computation.7 | async-start | bytes 1048576 | tf_op jit(solution)/shard_map/all_to_all | solution.py:35
  92.0 20.0 %all-to-all-start.11 = ((bf16[4,128,384]{2,1,0:T(8,128)(2,1)}), bf16[4,128,384]{2,1,0:T(8,128)(2,1)S(1)}, u32[]{:S(2)}, u32[]{:S(2)}) async-start(bf16[4,128,384]{2,1,0:T(8,128)(2,1)} %broadcast_in_dim.3), calls=%async_computation.11 | async-start | bytes 786432 | tf_op jit(solution)/shard_map/all_to_all | solution.py:19
  130.3 98.7 %all-to-all-start.5 = ((bf16[16,4,4,4096]{3,2,1,0:T(4,128)(2,1)}), bf16[16,4,4,4096]{3,2,1,0:T(4,128)(2,1)S(1)}, u32[]{:S(2)}, u32[]{:S(2)}) async-start(bf16[16,4,4,4096]{3,2,1,0:T(4,128)(2,1)} %stack.31), calls=%async_computation.5 | async-start | bytes 4194304 | tf_op jit(solution)/shard_map/all_to_all | solution.py:35
  232.7 48.9 %all-to-all-start.9 = ((bf16[4,32,4,4096]{3,1,2,0:T(8,128)(2,1)}), bf16[4,32,4,4096]{3,1,2,0:T(8,128)(2,1)}, u32[]{:S(2)}, u32[]{:S(2)}) async-start(bf16[4,32,4,4096]{3,1,2,0:T(8,128)(2,1)} %stack.35), calls=%async_computation.9 | async-start | bytes 8388608 | tf_op jit(solution)/shard_map/all_to_all | solution.py:35
  241.4 89.3 %copy-start.2 = (bf16[4,2,4,4096]{3,2,1,0:T(4,128)(2,1)S(1)}, bf16[4,2,4,4096]{3,2,1,0:T(4,128)(2,1)}, u32[]{:S(2)}) copy-start(bf16[4,2,4,4096]{3,2,1,0:T(4,128)(2,1)} %all_to_all.88) | copy-start | bytes 786436
  334.7 201.9 %all-to-all-start.3 = ((bf16[16,8,4,4096]{3,2,1,0:T(4,128)(2,1)}), bf16[16,8,4,4096]{3,2,1,0:T(4,128)(2,1)}, u32[]{:S(2)}, u32[]{:S(2)}) async-start(bf16[16,8,4,4096]{3,2,1,0:T(4,128)(2,1)} %stack.29), calls=%async_computation.3 | async-start | bytes 8388608 | tf_op jit(solution)/shard_map/all_to_all | solution.py:35
  355.9 7.6 %copy-start.1 = (bf16[2,64,4,4096]{3,2,1,0:T(4,128)(2,1)S(1)}, bf16[2,64,4,4096]{3,2,1,0:T(4,128)(2,1)}, u32[]{:S(2)}) copy-start(bf16[2,64,4,4096]{3,2,1,0:T(4,128)(2,1)} %all_to_all.91) | copy-start | bytes 12582916
  566.9 111.9 %copy-start.3 = (f32[3]{0:T(128)S(1)}, f32[3]{0:T(128)}, u32[]{:S(2)}) copy-start(f32[3]{0:T(128)} %param.5) | copy-start | bytes 40
